TPU v7x, 32 devices: a whole 2x2x4 slice. The times are simulated.
32 devices in a mesh: dp: 8 (over y, x, core), tensor: 4 (over z).
Axes of the slice: x: 2, y: 2, z: 4, core: 2. Of those that a mesh axis runs over, the one named last changes fastest.
Arguments:
- tokens: bfloat16 [128, 8192], P('dp'), may hold values from -6 to 6
- norm_gain: bfloat16 [8192], replicated, may hold values from 0.099609375 to 1.8984375
- w_query: bfloat16 [8192, 8192], P('dp', 'tensor'), may hold values from -0.0625 to 0.0625
- w_key: bfloat16 [8192, 1024], P('dp', 'tensor'), may hold values from -0.0625 to 0.0625
- w_value: bfloat16 [8192, 1024], P('dp', 'tensor'), may hold values from -0.0625 to 0.0625
- check_column: bfloat16 [8192], replicated, may hold values from -6 to 6
- key_cache: bfloat16 [4096, 16, 8, 128], P('dp', None, 'tensor'), may hold values from -320 to 320
- value_cache: bfloat16 [4096, 16, 8, 128], P('dp', None, 'tensor'), may hold values from -6 to 6
- page_table: int32 [128, 32], P('dp'), may hold values from 0 to 511, as said below
- lengths: int32 [128], P('dp'), may hold values from 1 to 512, as said below
- tol_counts: int32 [128], replicated, may hold values from 0 to 7
Outputs:
- attention: bfloat16 [128, 8192], P('dp', 'tensor')
- excess: float32 [], replicated
Inputs may be any that keep to these rules, and one draw needn't show every extreme that they name: page_table holds pool pages of the index of dp that holds the sequence; the 16 sequences of one index of dp own distinct pages and together own all 512 of them. `lengths`: some sequence holds exactly 512 cached tokens.
All inputs are finite; a program needn't handle non-finite values.
Results may differ from a plain program's by a relative error of at most 0.007.
The roundings to bfloat16 on the way count: a program that leaves them out, or rounds other values in their place, can miss the bound.
Values may be sent and summed in bfloat16 or wider, within the bound.
A program may use at most 64 MiB of HBM per device.

v0:
```python
import math
import jax
import jax.numpy as jnp
from jax import lax
from jax.sharding import PartitionSpec as P

HQ = 64
KVH = 8
HD = 128
epsilon = 1e-06
rope_base = 1000000.0
tol_step = 0.25


def normalize(tokens, norm_gain):
    widened = tokens.astype(jnp.float32)
    mean_square = jnp.mean(widened * widened, axis=1, keepdims=True)
    return (widened * lax.rsqrt(mean_square + epsilon) * norm_gain.astype(jnp.float32)).astype(
        jnp.bfloat16
    )


def rotate(vectors, positions):
    half_width = vectors.shape[-1] // 2
    steps_index = jnp.arange(half_width, dtype=jnp.float32)
    inverse = rope_base ** (-2.0 * steps_index / vectors.shape[-1])
    angles = positions.astype(jnp.float32)[:, None] * inverse[None, :]
    cosine = jnp.cos(angles)[:, None, :]
    sine_part = jnp.sin(angles)[:, None, :]
    lower = vectors[..., :half_width]
    upper = vectors[..., half_width:]
    return jnp.concatenate(
        [lower * cosine - upper * sine_part, upper * cosine + lower * sine_part], axis=-1
    )


def attend(query_heads, cached_keys, cached_values, key_new, value_new, lengths):
    score_scale = query_heads.shape[-1] ** (-0.5)
    scores = (
        jnp.einsum("skgd,sckd->skgc", query_heads, cached_keys, preferred_element_type=jnp.float32)
        * score_scale
    )
    new_score = (
        jnp.einsum("skgd,skd->skg", query_heads, key_new, preferred_element_type=jnp.float32)
        * score_scale
    )
    live_mask = (jnp.arange(cached_keys.shape[1])[None, :] < lengths[:, None])[:, None, None, :]
    masked = jnp.where(live_mask, scores, -jnp.inf)
    peak_score = jnp.maximum(jnp.max(masked, axis=-1), new_score)
    weights = jnp.exp(masked - peak_score[..., None])
    new_weight = jnp.exp(new_score - peak_score)
    denominator = jnp.sum(weights, axis=-1) + new_weight
    rounded_new = lax.optimization_barrier(new_weight.astype(jnp.bfloat16)).astype(jnp.float32)
    mixed_heads = jnp.einsum(
        "skgc,sckd->skgd",
        weights.astype(jnp.bfloat16),
        cached_values,
        preferred_element_type=jnp.float32,
    )
    mixed_heads = (
        mixed_heads + rounded_new[..., None] * value_new.astype(jnp.float32)[:, :, None, :]
    )
    return mixed_heads / denominator[..., None]


def body(
    tokens,
    norm_gain,
    w_query,
    w_key,
    w_value,
    check_column,
    key_cache,
    value_cache,
    page_table,
    lengths,
    tol_counts,
):
    seq_rows = tokens.shape[0]
    head_size = key_cache.shape[-1]
    normed = normalize(tokens, norm_gain)
    spread = lax.all_to_all(normed, "dp", split_axis=1, concat_axis=0, tiled=True)
    projected = lax.psum_scatter(
        jnp.concatenate(
            [
                jnp.dot(spread, w_query, preferred_element_type=jnp.float32),
                jnp.dot(spread, w_key, preferred_element_type=jnp.float32),
                jnp.dot(spread, w_value, preferred_element_type=jnp.float32),
            ],
            axis=1,
        ),
        "dp",
        scatter_dimension=0,
        tiled=True,
    )
    column_count = (HQ + 2 * KVH) * HD
    local_sums = jnp.sum(projected, axis=1)
    check_sums = jnp.dot(normed, check_column, preferred_element_type=jnp.float32)
    all_rows = seq_rows * lax.axis_size("dp")
    block_total = lax.psum(local_sums, "tensor")
    residual = (block_total - check_sums) / math.sqrt(column_count)
    own_counts = lax.dynamic_slice_in_dim(tol_counts, lax.axis_index("dp") * seq_rows, seq_rows, 0)
    token_excess = jnp.maximum(jnp.abs(residual) - tol_step * own_counts.astype(jnp.float32), 0.0)
    excess = lax.psum(jnp.sum(token_excess), "dp") / math.sqrt(all_rows)
    query_width = w_query.shape[1]
    kv_width = w_key.shape[1]
    heads_here = query_width // head_size
    kv_here = kv_width // head_size
    group_size = heads_here // kv_here
    query_heads = rotate(
        projected[:, :query_width].reshape(seq_rows, heads_here, head_size), lengths
    ).astype(jnp.bfloat16)
    key_new = rotate(
        projected[:, query_width : query_width + kv_width].reshape(seq_rows, kv_here, head_size),
        lengths,
    ).astype(jnp.bfloat16)
    value_new = (
        projected[:, query_width + kv_width :]
        .reshape(seq_rows, kv_here, head_size)
        .astype(jnp.bfloat16)
    )
    context = page_table.shape[1] * key_cache.shape[1]
    cached_keys = key_cache[page_table].reshape(seq_rows, context, kv_here, head_size)
    cached_values = value_cache[page_table].reshape(seq_rows, context, kv_here, head_size)
    mixed_heads = attend(
        query_heads.reshape(seq_rows, kv_here, group_size, head_size),
        cached_keys,
        cached_values,
        key_new,
        value_new,
        lengths,
    )
    attention = mixed_heads.reshape(seq_rows, heads_here * head_size).astype(jnp.bfloat16)
    return (attention, excess)


def solution(mesh):
    return jax.shard_map(
        body,
        mesh=mesh,
        in_specs=(
            P("dp", None),
            P(),
            P("dp", "tensor"),
            P("dp", "tensor"),
            P("dp", "tensor"),
            P(),
            P("dp", None, "tensor", None),
            P("dp", None, "tensor", None),
            P("dp", None),
            P("dp"),
            P(),
        ),
        out_specs=(P("dp", "tensor"), P()),
        check_vma=False,
    )
```

profile of v0, /device:TPU:0, one launch (start us, length us, event | category | flops | bytes accessed | tf_op | source)
XLA Modules:
  0.0 112.8 jit_solution(3940813790565365840)
XLA Ops:
  7.2 0.0 copy-start
  7.2 0.0 copy-start.2
  7.2 0.0 reduce-scatter.2.cloned.1.call-start
  7.2 0.8 convert_element_type.51
  8.0 1.1 fusion.25
  9.2 1.1 fusion.27
  10.3 11.9 %all_to_all.19 = bf16[16,8,1024]{2,0,1:T(8,128)(2,1)S(1)} all-to-all(bf16[16,8,1024]{2,0,1:T(8,128)(2,1)S(1)} %bitcast.54), channel_id=1, replica_groups=mesh['dp'=8,'tensor'=4] {'dp'}, dimensions={1} | all-to-all | bytes 524288 | tf_op jit(solution)/shard_map/all_to_all | solution.py:82
  22.2 2.9 %fusion.42 = f32[128,2048]{1,0:T(8,128)S(1)} fusion(bf16[128,1024]{1,0:T(8,128)(2,1)S(1)} %bitcast.49, bf16[1024,2048]{1,0:T(8,128)(2,1)} %param.13), kind=kOutput, calls=%fused_computation.57 | convolution fusion | flops 536870912 | bytes 5505024 | tf_op jit(solution)/shard_map/dot_general | solution.py:86
  25.1 0.0 copy-done
  25.1 0.0 copy-start.5
  25.1 0.0 copy-start.4
  25.1 0.2 fusion.43
  25.4 0.0 copy-done.2
  25.4 0.2 fusion.44
  25.7 1.3 %pad_maximum_fusion = f32[128,2560]{1,0:T(8,128)} fusion(f32[128,256]{1,0:T(8,128)S(1)} %fusion.44, f32[128,256]{1,0:T(8,128)S(1)} %fusion.43, f32[128,2048]{1,0:T(8,128)S(1)} %fusion.42), kind=kLoop, calls=%fused_computation.6 | loop fusion | flops 655360 | bytes 2621440 | tf_op jit(solution)/shard_map/concatenate | solution.py:84
  26.9 0.0 reduce-scatter.2.cloned.1.call-update
  26.9 0.0 copy-done.5
  27.0 0.0 copy-done.4
  27.0 0.1 reshape.122
  27.1 20.9 %gather_fusion = bf16[512,16,2,128]{3,2,1,0:T(2,128)(2,1)} fusion(bf16[512,16,2,128]{3,2,1,0:T(2,128)(2,1)} %param.17, s32[1024]{0:T(1024)S(1)} %pad_clamp_fusion), kind=kCustom, calls=%fused_computation | custom fusion | bytes 8390656 | tf_op jit(solution)/shard_map/gather | solution.py:123
  47.9 0.0 copy-start.3
  47.9 20.9 %gather_fusion.1 = bf16[512,16,2,128]{3,2,1,0:T(2,128)(2,1)} fusion(bf16[512,16,2,128]{3,2,1,0:T(2,128)(2,1)} %param.18, s32[1024]{0:T(1024)S(1)} %pad_clamp_fusion), kind=kCustom, calls=%fused_computation.1 | custom fusion | bytes 8390656 | tf_op jit(solution)/shard_map/gather | solution.py:124
  68.8 0.0 copy-done.3
  68.9 0.1 iota_compare_fusion
  68.9 0.1 multiply_cosine_fusion
  69.1 0.0 reduce-scatter.2.cloned.1.call-done
  69.1 0.0 copy-start.1
  69.1 0.8 slice.36
  69.9 0.9 slice_bitcast_fusion
  70.9 0.1 subtract_convert_fusion.1
  71.0 0.1 fusion.32
  71.1 0.1 maximum_bitcast_fusion
  71.2 0.2 fusion.34
  71.4 3.5 %fusion.41 = (f32[16,2,8]{2,1,0:T(2,128)S(1)}, f32[16,2,8,512]{3,2,1,0:T(8,128)S(1)}) fusion(bf16[16,512,2,128]{3,2,1,0:T(2,128)(2,1)} %bitcast.47, bf16[16,2,8,64]{3,2,1,0:T(8,128)(2,1)S(1)} %get-tuple-element.3, bf16[16,2,8,64]{3,2,1,0:T(8,128)(2,1)S(1)} %get-tuple-element.2, pred[16,512]{1,0:T(8,128)(4,1)S(1)} %iota_compare_fusion), kind=kOutput, calls=%fused_computation.56 | convolution fusion | flops 34078464 | bytes 4793344 | tf_op jit(solution)/shard_map/skgd,sckd->skgc/dot_general | solution.py:40
  74.9 0.0 copy-start.6
  74.9 0.2 fusion.28
  75.2 0.0 copy-done.1
  75.3 0.1 reduce_sum.38
  75.4 12.0 %psum.14 = f32[16]{0:T(128)S(1)} all-reduce(f32[16]{0:T(128)S(1)} %reduce_sum.38), channel_id=1, replica_groups=mesh['dp'=8,'tensor'=4] {'tensor'}, use_global_device_ids=true, to_apply=%region_5.0 | all-reduce | flops 16 | bytes 128 | tf_op jit(solution)/shard_map/psum | solution.py:100
  87.4 2.9 %fusion.16 = bf16[16,2,8,128]{3,2,1,0:T(8,128)(2,1)S(1)} fusion(bf16[16,512,2,128]{3,2,1,0:T(2,128)(2,1)} %bitcast.48, f32[16,2,8,512]{3,2,1,0:T(8,128)S(1)} %get-tuple-element.11, f32[16,2,8]{2,1,0:T(2,128)S(1)} %multiply_maximum_fusion, f32[16,2,8]{2,1,0:T(2,128)S(1)} %get-tuple-element.5, f32[16,2,128]{2,1,0:T(2,128)S(1)} %reshape.119, ...), kind=kOutput, calls=%fused_computation.11 | convolution fusion | flops 33947648 | bytes 4803584 | tf_op jit(solution)/shard_map/skgc,sckd->skgd/dot_general | solution.py:54
  90.3 0.0 copy-done.6
  90.3 0.8 fusion.24
  91.1 0.6 copy.49
  91.7 12.4 %psum.15 = f32[]{:T(128)} all-reduce(f32[]{:T(128)} %fusion.24), channel_id=1, replica_groups=mesh['dp'=8,'tensor'=4] {'dp'}, use_global_device_ids=true, to_apply=%region_7.8 | all-reduce | flops 1 | bytes 8 | tf_op jit(solution)/shard_map/psum | solution.py:104
  (14 shorter events, 0.2 us)
Async XLA Ops:
  7.2 18.0 %copy-start = (bf16[1024,256]{1,0:T(8,128)(2,1)S(1)}, bf16[1024,256]{1,0:T(8,128)(2,1)}, u32[]{:S(2)}) copy-start(bf16[1024,256]{1,0:T(8,128)(2,1)} %param.14) | copy-start | bytes 1572868
  7.2 18.2 %copy-start.2 = (bf16[1024,256]{1,0:T(8,128)(2,1)S(1)}, bf16[1024,256]{1,0:T(8,128)(2,1)}, u32[]{:S(2)}) copy-start(bf16[1024,256]{1,0:T(8,128)(2,1)} %param.15) | copy-start | bytes 1572868
  7.2 61.9 %reduce-scatter.2.cloned.1.call-start = ((), (), s32[]{:S(2)}) async-start(), calls=%async_computation.2 | async-start | bytes 1474560 | tf_op jit(solution)/shard_map/reduce_scatter | solution.py:83
  25.1 1.8 %copy-start.5 = (s32[16]{0:T(128)S(1)}, s32[16]{0:T(128)}, u32[]{:S(2)}) copy-start(s32[16]{0:T(128)} %param.20) | copy-start | bytes 196
  25.1 1.8 %copy-start.4 = (s32[16,32]{1,0:T(8,128)S(1)}, s32[16,32]{1,0:T(8,128)}, u32[]{:S(2)}) copy-start(s32[16,32]{1,0:T(8,128)} %param.19) | copy-start | bytes 6148
  47.9 20.9 %copy-start.3 = (bf16[8192]{0:T(1024)(128)(2,1)S(1)}, bf16[8192]{0:T(1024)(128)(2,1)}, u32[]{:S(2)}) copy-start(bf16[8192]{0:T(1024)(128)(2,1)} %param.16) | copy-start | bytes 49156
  69.1 6.1 %copy-start.1 = (f32[16,2560]{1,0:T(8,128)S(1)}, f32[16,2560]{1,0:T(8,128)}, u32[]{:S(2)}) copy-start(f32[16,2560]{1,0:T(8,128)} %reduce-scatter.2.cloned.1.call-done) | copy-start | bytes 491524
  74.9 15.4 %copy-start.6 = (s32[128]{0:T(128)S(1)}, s32[128]{0:T(128)}, u32[]{:S(2)}) copy-start(s32[128]{0:T(128)} %param.21) | copy-start | bytes 1540
Sparse Core Ops, SparseCore 0:
  27.1 36.5 reduce-scatter.1
where the time goes:
time: 113 us
  local copies, waits for them, and re-layouts  44.3 us (39%)
  blocking collectives  36.3 us (32%)
  between operations  16.1 us (14%)
  matrix products  10.8 us (10%)
  other arithmetic  5.21 us (5%)
    gather x1, local copies, waits for them, and re-layouts, body(): value_cache[page_table].reshape(seq_rows, context, kv_here, head_size)  20.9 us
    gather x1, local copies, waits for them, and re-layouts, body(): key_cache[page_table].reshape(seq_rows, context, kv_here, head_size)  20.9 us
    psum x1, blocking collectives, body(): excess = lax.psum(jnp.sum(token_excess), 'dp') / math.sqrt(all_rows)  12.4 us
    psum x1, blocking collectives, body(): block_total = lax.psum(local_sums, 'tensor')  12 us
    all_to_all x1, blocking collectives, body(): lax.all_to_all(normed, 'dp', split_axis=1, concat_axis=0, tiled=True)  11.9 us
    dot_general x1, matrix products, attend(): jnp.einsum('skgd,sckd->skgc', query_heads, cached_keys, preferred_element...  3.52 us
    dot_general x1, matrix products, body(): jnp.dot(spread, w_query, preferred_element_type=jnp.float32)  2.92 us
    dot_general x1, matrix products, attend(): jnp.einsum('skgc,sckd->skgd', weights.astype(jnp.bfloat16), cached_values...  2.89 us
  transfers between devices with their start and end apart: 1, of which 0 were waited for; matrix products, arithmetic and copies ran while one was open for 37% of the time, Pallas kernels for 0%

commit v1 on v0

--- a/solution.py
+++ b/solution.py
@@ -97,7 +97,7 @@
     local_sums = jnp.sum(projected, axis=1)
     check_sums = jnp.dot(normed, check_column, preferred_element_type=jnp.float32)
     all_rows = seq_rows * lax.axis_size("dp")
-    block_total = lax.psum(local_sums, "tensor")
+    block_total = jnp.sum(lax.all_gather(local_sums, "tensor"), axis=0)
     residual = (block_total - check_sums) / math.sqrt(column_count)
     own_counts = lax.dynamic_slice_in_dim(tol_counts, lax.axis_index("dp") * seq_rows, seq_rows, 0)
     token_excess = jnp.maximum(jnp.abs(residual) - tol_step * own_counts.astype(jnp.float32), 0.0)

time: 113 us -> 115 us (1.018)
    psum x1 -> x0, blocking collectives: 12 us -> none  [body(): block_total = lax.psum(local_sums, 'tensor')]
    unnamed x0 -> x1, blocking collectives: none -> 11.9 us
    unnamed x18 -> x23, local copies, waits for them, and re-layouts: 1.65 us -> 2.48 us
where the time goes in v1:
time: 115 us; the launch traced here: 114 us
  local copies, waits for them, and re-layouts  45.2 us (39%)
  blocking collectives  36.3 us (32%)
  between operations  16.7 us (15%)
  matrix products  10.8 us (9%)
  other arithmetic  5.24 us (5%)
    gather x1, local copies, waits for them, and re-layouts, body(): value_cache[page_table].reshape(seq_rows, context, kv_here, head_size)  20.9 us
    gather x1, local copies, waits for them, and re-layouts, body(): key_cache[page_table].reshape(seq_rows, context, kv_here, head_size)  20.9 us
    psum x1, blocking collectives, body(): excess = lax.psum(jnp.sum(token_excess), 'dp') / math.sqrt(all_rows)  12.4 us
    unnamed x1, blocking collectives  11.9 us
    all_to_all x1, blocking collectives, body(): lax.all_to_all(normed, 'dp', split_axis=1, concat_axis=0, tiled=True)  11.9 us
    dot_general x1, matrix products, attend(): jnp.einsum('skgd,sckd->skgc', query_heads, cached_keys, preferred_element...  3.52 us
    dot_general x1, matrix products, body(): jnp.dot(spread, w_query, preferred_element_type=jnp.float32)  2.92 us
    dot_general x1, matrix products, attend(): jnp.einsum('skgc,sckd->skgd', weights.astype(jnp.bfloat16), cached_values...  2.89 us
  transfers between devices with their start and end apart: 1, of which 0 were waited for; matrix products, arithmetic and copies ran while one was open for 37% of the time, Pallas kernels for 0%

profile of v1, /device:TPU:0, one launch (start us, length us, event | category | flops | bytes accessed | tf_op | source)
XLA Modules:
  0.0 114.4 jit_solution(8122586701614347097)
XLA Ops:
  7.2 0.0 copy-start
  7.2 0.0 copy-start.2
  7.2 0.0 reduce-scatter.2.cloned.1.call-start
  7.2 0.8 convert_element_type.51
  8.0 1.1 fusion.25
  9.2 1.1 fusion.27
  10.3 11.9 %all_to_all.19 = bf16[16,8,1024]{2,0,1:T(8,128)(2,1)S(1)} all-to-all(bf16[16,8,1024]{2,0,1:T(8,128)(2,1)S(1)} %bitcast.55), channel_id=1, replica_groups=mesh['dp'=8,'tensor'=4] {'dp'}, dimensions={1} | all-to-all | bytes 524288 | tf_op jit(solution)/shard_map/all_to_all | solution.py:82
  22.2 2.9 %fusion.42 = f32[128,2048]{1,0:T(8,128)S(1)} fusion(bf16[128,1024]{1,0:T(8,128)(2,1)S(1)} %bitcast.50, bf16[1024,2048]{1,0:T(8,128)(2,1)} %param.13), kind=kOutput, calls=%fused_computation.57 | convolution fusion | flops 536870912 | bytes 5505024 | tf_op jit(solution)/shard_map/dot_general | solution.py:86
  25.1 0.0 copy-done
  25.1 0.0 copy-start.5
  25.1 0.0 copy-start.4
  25.1 0.2 fusion.43
  25.4 0.0 copy-done.2
  25.4 0.2 fusion.44
  25.7 1.3 %pad_maximum_fusion = f32[128,2560]{1,0:T(8,128)} fusion(f32[128,256]{1,0:T(8,128)S(1)} %fusion.44, f32[128,256]{1,0:T(8,128)S(1)} %fusion.43, f32[128,2048]{1,0:T(8,128)S(1)} %fusion.42), kind=kLoop, calls=%fused_computation.6 | loop fusion | flops 655360 | bytes 2621440 | tf_op jit(solution)/shard_map/concatenate | solution.py:84
  26.9 0.0 reduce-scatter.2.cloned.1.call-update
  26.9 0.0 copy-done.5
  27.0 0.0 copy-done.4
  27.0 0.1 reshape.122
  27.1 20.9 %gather_fusion = bf16[512,16,2,128]{3,2,1,0:T(2,128)(2,1)} fusion(bf16[512,16,2,128]{3,2,1,0:T(2,128)(2,1)} %param.17, s32[1024]{0:T(1024)S(1)} %pad_clamp_fusion), kind=kCustom, calls=%fused_computation | custom fusion | bytes 8390656 | tf_op jit(solution)/shard_map/gather | solution.py:123
  47.9 0.0 copy-start.3
  47.9 0.0 copy-start.7
  47.9 20.9 %gather_fusion.1 = bf16[512,16,2,128]{3,2,1,0:T(2,128)(2,1)} fusion(bf16[512,16,2,128]{3,2,1,0:T(2,128)(2,1)} %param.18, s32[1024]{0:T(1024)S(1)} %pad_clamp_fusion), kind=kCustom, calls=%fused_computation.1 | custom fusion | bytes 8390656 | tf_op jit(solution)/shard_map/gather | solution.py:124
  68.8 0.0 copy-done.3
  68.9 0.0 copy-done.7
  68.9 0.6 dynamic-slice
  70.1 0.1 iota_compare_fusion
  70.2 0.1 multiply_cosine_fusion
  70.3 0.0 reduce-scatter.2.cloned.1.call-done
  70.4 0.0 copy-start.1
  70.4 0.8 slice.36
  71.2 0.9 slice_bitcast_fusion
  72.1 0.1 subtract_convert_fusion.1
  72.2 0.1 fusion.32
  72.3 0.1 maximum_bitcast_fusion
  72.4 0.2 fusion.34
  72.6 3.5 %fusion.41 = (f32[16,2,8]{2,1,0:T(2,128)S(1)}, f32[16,2,8,512]{3,2,1,0:T(8,128)S(1)}) fusion(bf16[16,512,2,128]{3,2,1,0:T(2,128)(2,1)} %bitcast.48, bf16[16,2,8,64]{3,2,1,0:T(8,128)(2,1)S(1)} %get-tuple-element.3, bf16[16,2,8,64]{3,2,1,0:T(8,128)(2,1)S(1)} %get-tuple-element.2, pred[16,512]{1,0:T(8,128)(4,1)S(1)} %iota_compare_fusion), kind=kOutput, calls=%fused_computation.56 | convolution fusion | flops 34078464 | bytes 4793344 | tf_op jit(solution)/shard_map/skgd,sckd->skgc/dot_general | solution.py:40
  76.2 0.0 copy-start.6
  76.2 0.2 fusion.28
  76.5 0.0 copy-done.1
  76.5 0.1 reduce_sum.47
  76.7 0.2 dynamic-update-slice
  76.9 11.9 %all-reduce = f32[64]{0:T(128)S(1)} all-reduce(f32[64]{0:T(128)S(1)} %dynamic-update-slice), channel_id=2, replica_groups=mesh['dp'=8,'tensor'=4] {'tensor'}, use_global_device_ids=true, to_apply=%add | all-reduce | flops 64 | bytes 512
  88.9 0.1 reshape.136
  89.0 2.9 %fusion.16 = bf16[16,2,8,128]{3,2,1,0:T(8,128)(2,1)S(1)} fusion(bf16[16,512,2,128]{3,2,1,0:T(2,128)(2,1)} %bitcast.49, f32[16,2,8,512]{3,2,1,0:T(8,128)S(1)} %get-tuple-element.11, f32[16,2,8]{2,1,0:T(2,128)S(1)} %multiply_maximum_fusion, f32[16,2,8]{2,1,0:T(2,128)S(1)} %get-tuple-element.5, f32[16,2,128]{2,1,0:T(2,128)S(1)} %reshape.119, ...), kind=kOutput, calls=%fused_computation.11 | convolution fusion | flops 33947648 | bytes 4803584 | tf_op jit(solution)/shard_map/skgc,sckd->skgd/dot_general | solution.py:54
  91.9 0.0 copy-done.6
  91.9 0.8 fusion.24
  92.7 0.6 copy.49
  93.3 12.4 %psum.7 = f32[]{:T(128)} all-reduce(f32[]{:T(128)} %fusion.24), channel_id=1, replica_groups=mesh['dp'=8,'tensor'=4] {'dp'}, use_global_device_ids=true, to_apply=%region_7.8 | all-reduce | flops 1 | bytes 8 | tf_op jit(solution)/shard_map/psum | solution.py:104
  (16 shorter events, 0.2 us)
Async XLA Ops:
  7.2 18.0 %copy-start = (bf16[1024,256]{1,0:T(8,128)(2,1)S(1)}, bf16[1024,256]{1,0:T(8,128)(2,1)}, u32[]{:S(2)}) copy-start(bf16[1024,256]{1,0:T(8,128)(2,1)} %param.14) | copy-start | bytes 1572868
  7.2 18.2 %copy-start.2 = (bf16[1024,256]{1,0:T(8,128)(2,1)S(1)}, bf16[1024,256]{1,0:T(8,128)(2,1)}, u32[]{:S(2)}) copy-start(bf16[1024,256]{1,0:T(8,128)(2,1)} %param.15) | copy-start | bytes 1572868
  7.2 63.2 %reduce-scatter.2.cloned.1.call-start = ((), (), s32[]{:S(2)}) async-start(), calls=%async_computation.2 | async-start | bytes 1474560 | tf_op jit(solution)/shard_map/reduce_scatter | solution.py:83
  25.1 1.8 %copy-start.5 = (s32[16]{0:T(128)S(1)}, s32[16]{0:T(128)}, u32[]{:S(2)}) copy-start(s32[16]{0:T(128)} %param.20) | copy-start | bytes 196
  25.1 1.8 %copy-start.4 = (s32[16,32]{1,0:T(8,128)S(1)}, s32[16,32]{1,0:T(8,128)}, u32[]{:S(2)}) copy-start(s32[16,32]{1,0:T(8,128)} %param.19) | copy-start | bytes 6148
  47.9 20.9 %copy-start.3 = (bf16[8192]{0:T(1024)(128)(2,1)S(1)}, bf16[8192]{0:T(1024)(128)(2,1)}, u32[]{:S(2)}) copy-start(bf16[8192]{0:T(1024)(128)(2,1)} %param.16) | copy-start | bytes 49156
  47.9 20.9 %copy-start.7 = (u32[32]{0:T(128)S(1)}, u32[32]{0:T(128)}, u32[]{:S(2)}) copy-start(u32[32]{0:T(128)} %constant.46) | copy-start | bytes 388
  70.4 6.1 %copy-start.1 = (f32[16,2560]{1,0:T(8,128)S(1)}, f32[16,2560]{1,0:T(8,128)}, u32[]{:S(2)}) copy-start(f32[16,2560]{1,0:T(8,128)} %reduce-scatter.2.cloned.1.call-done) | copy-start | bytes 491524
  76.2 15.7 %copy-start.6 = (s32[128]{0:T(128)S(1)}, s32[128]{0:T(128)}, u32[]{:S(2)}) copy-start(s32[128]{0:T(128)} %param.21) | copy-start | bytes 1540
Sparse Core Ops, SparseCore 0:
  27.1 36.5 reduce-scatter.1
